TPU v7x, 32 devices: a whole 2x2x4 slice. The times are simulated.
32 devices in a mesh: outer: 4 (over z), inner: 8 (over y, x, core).
Axes of the slice: x: 2, y: 2, z: 4, core: 2. Of those that a mesh axis runs over, the one named last changes fastest.
Arguments:
- g_emb: float32 [32, 4096, 768], P(('outer', 'inner'))
- g_qkv: float32 [32, 1, 768, 2304], P(('outer', 'inner'))
- g_o: float32 [32, 1, 768, 768], P(('outer', 'inner'))
- g_w1: float32 [32, 1, 768, 2048], P(('outer', 'inner'))
- g_w2: float32 [32, 1, 2048, 768], P(('outer', 'inner'))
- g_bqkv: float32 [32, 1, 2304], P(('outer', 'inner'))
- g_b1: float32 [32, 1, 2048], P(('outer', 'inner'))
- g_dvec: float32 [32, 1, 6, 768], P(('outer', 'inner'))
- m: float32 [8659712], P(('outer', 'inner'))
- v: float32 [8659712], P(('outer', 'inner'))
- w: float32 [8659712], P(('outer', 'inner'))
- lr: float32 [], replicated
- beta1: float32 [], replicated
- beta2: float32 [], replicated
- eps: float32 [], replicated
- step: int32 [], replicated
Outputs:
- output 1: float32 [8659712], P(('outer', 'inner'))
- output 2: float32 [8659712], P(('outer', 'inner'))
- output 3: float32 [8659712], P(('outer', 'inner'))
- output 4: bfloat16 [4096, 768], replicated
- output 5: bfloat16 [1, 768, 2304], replicated
- output 6: bfloat16 [1, 768, 768], replicated
- output 7: bfloat16 [1, 768, 2048], replicated
- output 8: bfloat16 [1, 2048, 768], replicated
- output 9: bfloat16 [1, 2304], replicated
- output 10: bfloat16 [1, 2048], replicated
- output 11: bfloat16 [1, 6, 768], replicated
All inputs are finite; a program needn't handle non-finite values.
Results may differ from a plain program's by a relative error of at most 0.001.
Values are sent between devices in bfloat16 or wider.
A program may use at most 1 GiB of HBM per device.

v0:
```python
import math
import jax
import jax.numpy as jnp
from jax import lax
from jax.sharding import PartitionSpec as P

AXES = ("outer", "inner")


def adam_update(g, m, v, w, lr, beta1, beta2, eps, step):
    t = step.astype(jnp.float32)
    m_new = beta1 * m + (1.0 - beta1) * g
    v_new = beta2 * v + (1.0 - beta2) * (g * g)
    m_hat = m_new / (1.0 - beta1 ** t)
    v_hat = v_new / (1.0 - beta2 ** t)
    w_new = w - lr * m_hat / (jnp.sqrt(v_hat) + eps)
    return m_new, v_new, w_new


def restore(flat, shapes):
    outs = []
    start = 0
    for shape in shapes:
        n = math.prod(shape)
        outs.append(flat[start:start + n].reshape(shape))
        start = start + n
    return tuple(outs)


def solution(mesh):
    p = mesh.shape["outer"] * mesh.shape["inner"]

    def body(g_emb, g_qkv, g_o, g_w1, g_w2, g_bqkv, g_b1, g_dvec, m, v, w, lr, beta1, beta2, eps, step):
        grads = (g_emb, g_qkv, g_o, g_w1, g_w2, g_bqkv, g_b1, g_dvec)
        shapes = tuple(x.shape[1:] for x in grads)
        local = jnp.concatenate([x.reshape(-1) for x in grads])
        g = lax.psum_scatter(local, AXES, scatter_dimension=0, tiled=True) / p
        m_new, v_new, w_new = adam_update(g, m, v, w, lr, beta1, beta2, eps, step)
        wb = lax.all_gather(w_new.astype(jnp.bfloat16), AXES, axis=0, tiled=True)
        return (m_new, v_new, w_new) + restore(wb, shapes)

    g3 = P(AXES, None, None)
    g4 = P(AXES, None, None, None)
    flat = P(AXES)
    rep = P()
    in_specs = (g3, g4, g4, g4, g4, g3, g3, g4, flat, flat, flat, rep, rep, rep, rep, rep)
    out_specs = (flat, flat, flat, rep, rep, rep, rep, rep, rep, rep, rep)
    return jax.shard_map(body, mesh=mesh, in_specs=in_specs, out_specs=out_specs, check_vma=False)
```

profile of v0, /device:TPU:0, one launch (start us, length us, event | category | flops | bytes accessed | tf_op | source)
XLA Modules:
  0.0 946.4 jit_solution(16370605506037876999)
XLA Ops:
  7.2 0.0 all-reduce.7.cloned.1.call-start
  7.2 13.3 %reshape.70 = f32[3145728]{0:T(1024)} reshape(f32[1,4096,768]{2,1,0:T(8,128)} %param.16) | data formatting | bytes 25165824 | tf_op jit(solution)/shard_map/reshape | solution.py:36
  20.6 10.0 %constant_dynamic-update-slice_fusion.7 = f32[8659712]{0:T(1024)} fusion(f32[3145728]{0:T(1024)} %reshape.70), kind=kLoop, calls=%fused_computation.10 | loop fusion | bytes 25165824
  30.6 0.0 copy-start.1
  30.6 8.1 reshape.71
  38.6 0.0 copy-done.1
  38.6 1.6 reshape.72
  40.2 6.9 copy.27
  47.1 0.0 copy-start.5
  47.1 0.0 copy-start.4
  47.1 6.9 reshape.74
  54.1 0.0 copy-done.5
  54.1 0.0 copy-done.4
  54.2 0.0 slice-start.2
  54.2 0.0 copy-start
  54.2 0.0 slice-start.3
  54.2 6.0 constant_dynamic-update-slice_fusion.6
  60.2 0.0 copy-done
  60.2 1.6 constant_dynamic-update-slice_fusion.5
  61.8 0.0 slice-start
  61.8 0.0 slice-done.2
  61.8 1.4 slice-done.3
  63.2 0.0 slice-start.1
  63.2 3.0 constant_dynamic-update-slice_fusion.4
  66.2 0.0 slice-done
  66.2 0.5 slice-done.1
  66.7 0.0 copy-start.6
  66.7 2.8 constant_dynamic-update-slice_fusion.3
  69.5 1.3 constant_dynamic-update-slice_fusion.2
  70.8 0.0 copy-done.6
  70.8 1.3 constant_dynamic-update-slice_fusion.1
  72.1 1.3 constant_dynamic-update-slice_fusion
  73.5 0.0 copy-start.2
  73.5 0.0 copy-start.3
  73.5 0.0 all-reduce.7.cloned.1.call-update
  73.5 0.0 all-reduce.5.cloned.1.call-start
  77.0 512.5 %all-reduce.7.cloned.1.call-done = f32[8659712]{0:T(1024)} async-done(((f32[8659712]{0:T(1024)}), f32[8659712]{0:T(1024)}) %all-reduce.7.cloned.1.call-update) | async-done | bytes 34638864
  589.6 0.0 copy-done.2
  589.6 0.0 copy-done.3
  589.6 4.3 fusion
  593.9 6.1 broadcast.2
  599.9 9.0 dynamic-update-slice
  608.9 0.0 all-reduce.5.cloned.1.call-update
  609.0 285.2 %all-reduce.5.cloned.1.call-done = bf16[8659712]{0:T(1024)(128)(2,1)} async-done(((bf16[8659712]{0:T(1024)(128)(2,1)}), bf16[8659712]{0:T(1024)(128)(2,1)}) %all-reduce.5.cloned.1.call-update) | async-done | bytes 17319440
  894.1 4.2 fusion.1
  898.3 5.8 reshape.81
  904.1 3.8 reshape.82
  907.9 6.5 slice.32
  914.4 11.6 %reshape.78 = bf16[4096,768]{1,0:T(8,128)(2,1)} reshape(bf16[3145728]{0:T(1024)(128)(2,1)} %slice.32) | data formatting | bytes 12582912 | tf_op jit(solution)/shard_map/reshape | solution.py:25
  925.9 0.0 slice-start.4
  925.9 2.0 slice-done.4
  927.9 5.1 reshape.79
  933.0 0.0 slice-start.5
  933.1 1.4 slice.34
  934.4 1.9 reshape.80
  936.3 0.7 slice.39
  937.0 0.6 reshape.85
  937.6 0.0 slice-done.5
  937.6 0.6 reshape.83
  938.2 0.7 slice.38
  938.9 0.6 reshape.84
  (5 shorter events, 0.1 us)
Async XLA Ops:
  7.2 582.4 %all-reduce.7.cloned.1.call-start = ((), (), s32[]{:S(2)}) async-start(), calls=%async_computation.1 | async-start | bytes 69279744
  30.6 8.1 copy-start.1
  47.1 6.9 copy-start.5
  47.1 7.0 copy-start.4
  54.2 7.6 slice-start.2
  54.2 6.0 copy-start
  54.2 9.0 slice-start.3
  61.8 4.4 slice-start
  63.2 3.5 slice-start.1
  66.7 4.2 copy-start.6
  73.5 516.1 %copy-start.2 = (f32[270616]{0:T(1024)S(1)}, f32[270616]{0:T(1024)}, u32[]{:S(2)}) copy-start(f32[270616]{0:T(1024)} %param.26) | copy-start | bytes 3247396
  73.5 516.1 %copy-start.3 = (f32[270616]{0:T(1024)S(1)}, f32[270616]{0:T(1024)}, u32[]{:S(2)}) copy-start(f32[270616]{0:T(1024)} %param.25) | copy-start | bytes 3247396
  73.5 820.7 %all-reduce.5.cloned.1.call-start = ((), (), s32[]{:S(2)}) async-start(), calls=%async_computation | async-start | bytes 34639872
  925.9 2.0 slice-start.4
  933.0 4.6 slice-start.5
Sparse Core Ops, SparseCore 0:
  73.6 515.9 all-reduce.6
  609.1 285.0 all-reduce.4
where the time goes:
time: 949 us; the launch traced here: 946 us
  waiting for transfers between devices  798 us (84%)
  local copies, waits for them, and re-layouts  127 us (13%)
  between operations  17.6 us (2%)
    unnamed x4, waiting for transfers between devices  798 us
    unnamed x32, local copies, waits for them, and re-layouts  50 us
    reshape x8, local copies, waits for them, and re-layouts, restore(): outs.append(flat[start:start + n].reshape(shape))  30 us
    reshape x5, local copies, waits for them, and re-layouts, body(): local = jnp.concatenate([x.reshape(-1) for x in grads])  29.9 us
  transfers between devices with their start and end apart: 2, of which 2 were waited for; matrix products, arithmetic and copies ran while one was open for 0% of the time, Pallas kernels for 0%

commit v1 on v0

v1 whole, which is shorter than its diff:
```python
import functools
import math

import jax
import jax.numpy as jnp
from jax import lax
from jax.experimental import pallas as pl
from jax.experimental.pallas import tpu as pltpu
from jax.sharding import PartitionSpec as P

AXES = ("outer", "inner")
MESH = pl.DeviceIdType.MESH
F32 = jnp.float32
BF16 = jnp.bfloat16

DEV = 32
SHARD = 270616
ROWS16 = 33827
TENSORS = ((0, 24576, 6), (24576, 38400, 18), (38400, 43008, 6), (43008, 55296, 16), (55296, 67584, 6))
TAIL0 = 67584
TAIL_ROWS = 80
LAST_ROW = 67654
NR = 2128
K = 19
NA, NB, NC = 40, 48, 24
CH = NA + NB + NC
SL = 4
S0 = 5
AHEAD = 2
HALO = 160
LOCPAD = 24
LROWS = 2120
FROWS = 2464


def win_start(r):
    if isinstance(r, int):
        return (r * ROWS16) // 256 * 16
    return lax.div(r * ROWS16, 256) * 16


def rows_of(r):
    lo, hi = win_start(r), win_start(r) + NR
    segs = []
    for i, (a, b, _) in enumerate(TENSORS + ((TAIL0, TAIL0 + TAIL_ROWS, 1),)):
        s, e = max(lo, a), min(hi, b)
        if s < e:
            segs.append((i, s - a, s - lo, e - s))
    return segs


def al(i, n, a=8):
    return pl.ds(pl.multiple_of(i, a), n)


def bits(w, n):
    out = []
    for _ in range(n):
        out.append(lax.rem(w, 2))
        w = lax.div(w, 2)
    return tuple(out[::-1])


def loop_add(dst, src, lead, n):
    def one(w, _):
        d, s = dst(w), src(w)
        for o in range(0, n, 8):
            d[pl.ds(o, 8), :] = d[pl.ds(o, 8), :] + s[pl.ds(o, 8), :]
        return 0

    lax.fori_loop(0, lead, one, 0)


def adam(g, m, v, w, sc):
    lr, b1, c1, b2, c2, i1, i2, eps = sc
    m2 = b1 * m + c1 * g
    v2 = b2 * v + c2 * (g * g)
    w2 = w - lr * (m2 * i1) / (jnp.sqrt(v2 * i2) + eps)
    return m2, v2, w2


H, L, Y, X = range(4)
ORDERS = ((X, Y, L, H), (Y, X, L, H), (L, H, X, Y))
PARTS = (NA, NB, NC)
STARTS = (0, NA, NA + NB)
NST = len(ORDERS[0])


def comm_kernel(sc_ref, e_ref, q_ref, o_ref, w1_ref, w2_ref, t_ref, m_ref, v_ref, w_ref, ag, out3, *scratch):
    bufs, scratch = scratch[:3 * NST], scratch[3 * NST:]
    (S, R0, LOC, F, TIL, HP, HN, GT, GP, GN, FG, WB,
     ld, s0s, s0r, rss, rsr, ags, agr, fws, fwr, lcl, mvs, hs, hr, osem) = scratch
    z = lax.axis_index(AXES[0])
    inner = lax.axis_index(AXES[1])
    h, l, y, x, c = bits(z, 2) + bits(inner, 3)
    me = (h, l, y, x)
    r = z * 8 + inner
    g_refs = (e_ref, q_ref, o_ref, w1_ref, w2_ref, t_ref)
    sc = [sc_ref[i] for i in range(8)]

    def flip(ax):
        p = [1 - b if i == ax else b for i, b in enumerate(me)]
        return p[H] * 2 + p[L], p[Y] * 4 + p[X] * 2 + c

    PEER = [flip(ax) for ax in range(4)]
    CORE = (z, inner + 1 - 2 * c)

    def device(i):
        i = lax.rem(i, DEV)
        return lax.div(i, 8), lax.rem(i, 8)

    NXT, PRV = device(r + 1), device(r + DEV - 1)

    def remote(src, dst, ss, rs, dev):
        return pltpu.make_async_remote_copy(src_ref=src, dst_ref=dst, send_sem=ss, recv_sem=rs,
                                            device_id=dev, device_id_type=MESH)

    def window_copies(w, q, make):
        segs = rows_of(w)
        off = q * CH
        if len(segs) == 1:
            i, a, _, _ = segs[0]
            make(g_refs[i].at[al(a + off, CH)], 0, CH)
            return
        for n, (i, a, b, size) in enumerate(segs):
            first, last = -(-b // CH), (b + size) // CH

            @pl.when(jnp.logical_and(q >= first, q < last))
            def _(i=i, a=a, b=b):
                make(g_refs[i].at[al(jnp.maximum(a + off - b, 0), CH)], 0, CH)

            if n + 1 < len(segs) and (b + size) % CH:
                edge, head = (b + size) // CH, (b + size) % CH
                j, a2, _, _ = segs[n + 1]

                @pl.when(q == edge)
                def _(i=i, a=a, size=size, head=head, j=j, a2=a2):
                    make(g_refs[i].at[pl.ds(a + size - head, head)], 0, head)
                    make(g_refs[j].at[pl.ds(a2, CH - head)], head, CH - head)

    def start0(q):
        slot = lax.rem(q, S0)
        for par in range(2):

            @pl.when(c == par)
            def _(par=par):
                for k in range(16):
                    idx = tuple(k >> i & 1 for i in (3, 2, 1, 0))

                    def send(src, o, n, idx=idx):
                        remote(src, R0.at[(slot,) + idx + (pl.ds(o, n),)], s0s.at[slot], s0r.at[slot], CORE).start()

                    def load(src, o, n, idx=idx):
                        pltpu.make_async_copy(src, S.at[idx + (al(q * CH + o, n),)], ld.at[slot]).start()

                    window_copies(2 * k + 1 - par, q, send)
                    window_copies(2 * k + par, q, load)

    def wait0(q):
        slot = lax.rem(q, S0)
        rows = S.at[:, :, :, :, al(q * CH, CH)]
        pltpu.make_async_copy(rows, rows, ld.at[slot]).wait()
        remote(R0.at[slot], R0.at[slot], s0s.at[slot], s0r.at[slot], CORE).wait()

    every = slice(None)

    def part(k, q):
        return al(q * CH + STARTS[k], PARTS[k])

    def where_rs(k, st, q, other):
        o = ORDERS[k]
        idx = [every] * 4
        for ax in o[:st]:
            idx[ax] = me[ax]
        idx[o[st]] = 1 - me[o[st]] if other else me[o[st]]
        return idx + [part(k, q)]

    def where_ag(k, st, q, other, core):
        o = ORDERS[k][::-1]
        idx = list(me)
        for ax in o[:st]:
            idx[ax] = every
        idx[o[st]] = 1 - me[o[st]] if other else me[o[st]]
        return tuple(idx + [core, part(k, q)])

    def rs_copy(k, st, q):
        s = lax.rem(q, SL)
        return remote(S.at[tuple(where_rs(k, st, q, True))], bufs[k * NST + st].at[s],
                      rss.at[k, st, s], rsr.at[k, st, s], PEER[ORDERS[k][st]])

    def ag_copy(k, st, q, recv):
        s = lax.rem(q, SL)
        dst = ag.at[where_ag(k, st, q, recv, c)]
        src = WB.at[part(k, q)] if st == 0 else dst
        return remote(src, dst, ags.at[k, st, s], agr.at[k, st, s], PEER[ORDERS[k][NST - 1 - st]])

    def fw_copy(k, st, q, core):
        s = lax.rem(q, SL)
        idx = list(where_ag(k, st, q, True, core))
        if st == 0:
            idx[ORDERS[k][NST - 1]] = every
        ref = ag.at[tuple(idx)]
        return remote(ref, ref, fws.at[k, st, s], fwr.at[k, st, s], CORE)

    def start(cp, q):
        @pl.when(q >= SL)
        def _():
            cp.wait_send()

        cp.start()

    def own_copy(q):
        return pltpu.make_async_copy(WB.at[al(q * CH, CH)], ag.at[me + (c, al(q * CH, CH))], lcl.at[lax.rem(q, SL)])

    def reduce_stage(k, st, q):
        rs_copy(k, st, q).wait_recv()
        s = lax.rem(q, SL)
        idx = where_rs(k, st, q, False)
        free = ORDERS[k][st + 1:]

        def dst(w):
            at = list(idx)
            for ax, b in zip(sorted(free), bits(w, len(free))):
                at[ax] = b
            return S.at[tuple(at)]

        loop_add(dst, lambda w: bufs[k * NST + st].at[(s,) + bits(w, len(free))], 2 ** len(free), PARTS[k])

    sr, srn = win_start(r), win_start(r + 1)
    delta = lax.rem(r * 24, 128)
    drow = lax.div(r * ROWS16, 16) - sr
    edge_n = lax.rem((r + 1) * 24, 128) + 128 * (lax.div((r + 1) * ROWS16, 16) - srn)
    nb = HALO + srn - sr
    lane = lax.broadcasted_iota(jnp.int32, (8, 128), 1)
    sub = lax.broadcasted_iota(jnp.int32, (8, 128), 0)

    def halo_copies():
        return [remote(F.at[:, al(nb - HALO, HALO + 16)], HP, hs.at[0], hr.at[0], NXT),
                remote(F.at[:, pl.ds(HALO, HALO + 16)], HN, hs.at[1], hr.at[1], PRV)]

    def state_copies():
        return [pltpu.make_async_copy(ref, LOC.at[k, pl.ds(LOCPAD, LROWS)], mvs.at[k])
                for k, ref in enumerate((m_ref, v_ref, w_ref))]

    def shift(ref, at, other, by, keep):
        a = pltpu.roll(ref[pl.ds(at, 8), :], by, 1)
        b = pltpu.roll(ref[pl.ds(at + other, 8), :], by, 1)
        return jnp.where(keep, a, b)

    def prepare1():
        for cp in state_copies():
            cp.wait()
        keep = lane >= delta

        def one(i, _):
            for j in range(4):
                at = i * 32 + j * 8
                for k in range(3):
                    F[k, al(HALO + at, 8), :] = shift(LOC.at[k], LOCPAD + at - drow, -1, delta, keep)
            return 0

        lax.fori_loop(0, (NR + 16) // 32, one, 0)
        for cp in halo_copies():
            cp.start()

    def blocks(first, last, body):
        for a, b, wt in TENSORS + ((TAIL0, TAIL0 + TAIL_ROWS, 1),):
            lo = lax.div(jnp.maximum(first - a, 0), 8 * wt)
            hi = lax.div(jnp.maximum(jnp.minimum(last, b) - a, 0) + 8 * wt - 1, 8 * wt)

            def one(i, _, a=a, wt=wt):
                body(a + i * 8 * wt, wt)
                return 0

            lax.fori_loop(lo, hi, one, 0)

    def prepare2():
        for cp in halo_copies():
            cp.wait()
        for k in range(3):
            for i in range(0, 16, 8):
                idx = (sub + i) * 128 + lane
                o = pl.ds(HALO + i, 8)
                F[k, o, :] = jnp.where(idx < drow * 128 + delta, HP[k, o, :], F[k, o, :])
                o = al(nb + i, 8)
                F[k, o, :] = jnp.where(idx >= edge_n, HN[k, pl.ds(i, 8), :], F[k, o, :])

        def one(i, _):
            for k in range(3):
                F[k, al(i * 16, 16), :] = HP[k, al(i * 16, 16), :]
                F[k, al(nb + 16 + i * 16, 16), :] = HN[k, al(16 + i * 16, 16), :]
            return 0

        lax.fori_loop(0, HALO // 16, one, 0)

        def permute(row, wt):
            at = row - sr + HALO
            for j in range(wt):
                for k in range(3):
                    TIL[k, al(at + 8 * j, 8), :] = (
                        F[k, pl.ds(at + j, 8, stride=wt), :] if wt > 1 else F[k, al(at, 8), :])

        blocks(sr, sr + NR, permute)

    def ghalo_copies():
        return [remote(GT.at[al(nb - HALO, HALO)], GP, hs.at[2], hr.at[2], NXT),
                remote(GT.at[pl.ds(HALO, HALO + 16)], GN, hs.at[3], hr.at[3], PRV)]

    def finish1():
        for cp in ghalo_copies():
            cp.start()

    def finish2():
        for cp in ghalo_copies():
            cp.wait()

        def put(i, _):
            GT[al(i * 16, 16), :] = GP[al(i * 16, 16), :]
            GT[al(HALO + NR + i * 16, 16), :] = GN[al(HALO + NR - nb + i * 16, 16), :]
            return 0

        lax.fori_loop(0, HALO // 16, put, 0)

        def permute(row, wt):
            at = row - sr + HALO
            for j in range(wt):
                v = GT[al(at + 8 * j, 8), :]
                if wt > 1:
                    FG[pl.ds(at + j, 8, stride=wt), :] = v
                else:
                    FG[al(at, 8), :] = v

        blocks(sr, srn + 16, permute)

    def out_copies():
        return [pltpu.make_async_copy(LOC.at[k, pl.ds(LOCPAD, LROWS)], out3.at[k], osem.at[k]) for k in range(3)]

    def finish3():
        back = lax.rem(128 - delta, 128)
        keep = lane < 128 - delta

        def one(i, _):
            for j in range(5):
                at = i * 40 + j * 8
                o = al(LOCPAD + at, 8)
                g = shift(FG, HALO + drow + at, 1, back, keep)
                new = adam(g, LOC[0, o, :], LOC[1, o, :], LOC[2, o, :], sc)
                for k in range(3):
                    LOC[k, o, :] = new[k]
            return 0

        lax.fori_loop(0, LROWS // 40, one, 0)
        for cp in out_copies():
            cp.start()

    for cp in state_copies():
        cp.start()
    for q in range(AHEAD):
        start0(q)

    def step(s, _):
        def at_stage(n, body):
            q = s - n

            @pl.when(jnp.logical_and(q >= 0, q < K))
            def _():
                body(q)

        def first(q):
            wait0(q)

            @pl.when(q + AHEAD < K)
            def _():
                start0(q + AHEAD)

            slot = lax.rem(q, S0)
            loop_add(lambda w: S.at[bits(w, 4) + (al(q * CH, CH),)], lambda w: R0.at[(slot,) + bits(w, 4)], 16, CH)
            for k in range(3):
                start(rs_copy(k, 0, q), q)

        at_stage(0, first)

        @pl.when(s == 1)
        def _():
            prepare1()

        for st in range(1, NST):
            def middle(q, st=st):
                for k in range(3):
                    reduce_stage(k, st - 1, q)
                    start(rs_copy(k, st, q), q)

            at_stage(st, middle)

        @pl.when(s == 2)
        def _():
            prepare2()

        def update(q):
            for k in range(3):
                reduce_stage(k, NST - 1, q)

            def one(i, _):
                o = al(q * CH + i * 16, 16)
                oh = al(HALO + q * CH + i * 16, 16)
                g = S[me + (o,)] * (1.0 / DEV)
                GT[oh, :] = g
                _, _, w2 = adam(g, TIL[0, oh, :], TIL[1, oh, :], TIL[2, oh, :], sc)
                WB[o, :] = w2.astype(BF16)
                return 0

            lax.fori_loop(0, CH // 16, one, 0)
            own_copy(q).start()
            for k in range(3):
                start(ag_copy(k, 0, q, False), q)

        at_stage(NST, update)

        for st in range(NST):
            def gather(q, st=st):
                if st == 0:
                    own_copy(q).wait()
                for k in range(3):
                    ag_copy(k, st, q, True).wait_recv()
                    if st + 1 < NST:
                        start(ag_copy(k, st + 1, q, False), q)
                    if st:
                        fw_copy(k, st - 1, q, 1 - c).wait_recv()
                    start(fw_copy(k, st, q, c), q)

            at_stage(NST + 1 + st, gather)

        def last(q):
            for k in range(3):
                fw_copy(k, NST - 1, q, 1 - c).wait_recv()

        at_stage(2 * NST + 1, last)

        for n, f in enumerate((finish1, finish2, finish3)):
            @pl.when(s == K + NST - 1 + n)
            def _(f=f):
                f()

        return 0

    lax.fori_loop(0, K + 2 * NST + 1, step, 0)

    def drain(i, _):
        q = K - SL + i
        for k in range(3):
            for st in range(NST):
                rs_copy(k, st, q).wait_send()
                ag_copy(k, st, q, False).wait_send()
                fw_copy(k, st, q, c).wait_send()
        return 0

    lax.fori_loop(0, SL, drain, 0)
    for cp in out_copies():
        cp.wait()


def unpack_kernel(ag, e_out, q_out, o_out, w1_out, w2_out, t_out, buf, isem, osem):
    outs = (e_out, q_out, o_out, w1_out, w2_out, t_out)
    depth = buf.shape[0]

    def get(r):
        return pltpu.make_async_copy(ag.at[tuple(r >> i & 1 for i in (4, 3, 2, 1, 0))], buf.at[r % depth], isem.at[r % depth])

    def puts(r):
        end = min(win_start(r + 1), TAIL0 + TAIL_ROWS) - win_start(r) if r + 1 < DEV else NR
        cps = []
        for n, (i, a, b, size) in enumerate(rows_of(r)):
            size = min(size, end - b)
            if size > 0:
                cps.append(pltpu.make_async_copy(buf.at[r % depth, pl.ds(b, size)], outs[i].at[pl.ds(a, size)],
                                                 osem.at[r % depth, n]))
        return cps

    for r in range(depth - 2):
        get(r).start()
    for r in range(DEV):
        get(r).wait()
        for cp in puts(r):
            cp.start()
        n = r + depth - 2
        if n < DEV:
            if n - depth >= 0:
                for cp in puts(n - depth):
                    cp.wait()
            get(n).start()
    for r in range(max(0, DEV - depth), DEV):
        for cp in puts(r):
            cp.wait()


def tiles(x, wt):
    rows = math.prod(x.shape) // (128 * wt)
    return x.reshape(rows // 8, 8, wt, 128).transpose(0, 2, 1, 3).reshape(rows * wt, 128)


def untiles(x, wt, shape):
    rows = x.shape[0] // wt
    return x.reshape(rows // 8, wt, 8, 128).transpose(0, 2, 1, 3).reshape(shape)


def solution(mesh):
    any_spec = pl.BlockSpec(memory_space=pl.ANY)
    dma = pltpu.SemaphoreType.DMA

    def vmem(*shape, dtype=F32):
        return pltpu.VMEM(shape + (128,), dtype)

    def body(g_emb, g_qkv, g_o, g_w1, g_w2, g_bqkv, g_b1, g_dvec, m, v, w, lr, beta1, beta2, eps, step):
        grads = (g_emb, g_qkv, g_o, g_w1, g_w2)
        shapes = tuple(g.shape[1:] for g in grads)
        big = [tiles(g, t[2]) for g, t in zip(grads, TENSORS)]
        tail = jnp.concatenate([g_bqkv.reshape(-1), g_b1.reshape(-1), g_dvec.reshape(-1)])
        tail = jnp.pad(tail, (0, TAIL_ROWS * 128 - tail.shape[0])).reshape(TAIL_ROWS, 128)
        t = step.astype(F32)
        sc = jnp.stack([lr, beta1, 1.0 - beta1, beta2, 1.0 - beta2,
                        1.0 / (1.0 - beta1 ** t), 1.0 / (1.0 - beta2 ** t), eps])
        state = [jnp.pad(a, (0, LROWS * 128 - SHARD)).reshape(LROWS, 128) for a in (m, v, w)]
        ag, out3 = pl.pallas_call(
            comm_kernel,
            out_shape=(jax.ShapeDtypeStruct((2, 2, 2, 2, 2, NR, 128), BF16), jax.ShapeDtypeStruct((3, LROWS, 128), F32)),
            in_specs=[pl.BlockSpec(memory_space=pltpu.SMEM)] + [any_spec] * 9,
            out_specs=(any_spec, any_spec),
            scratch_shapes=[vmem(SL, *[2] * (NST - 1 - st), n) for n in PARTS for st in range(NST)] + [
                vmem(2, 2, 2, 2, NR), vmem(S0, 2, 2, 2, 2, CH),
                vmem(3, 2176), vmem(3, FROWS), vmem(3, FROWS), vmem(3, HALO + 16), vmem(3, HALO + 16),
                vmem(NR + 2 * HALO), vmem(HALO), vmem(HALO + 16), vmem(NR + 2 * HALO), vmem(NR, dtype=BF16),
                dma((S0,)), dma((S0,)), dma((S0,))] + [dma((3, NST, SL)) for _ in range(6)] + [
                dma((SL,)), dma((3,)), dma((4,)), dma((4,)), dma((3,)),
            ],
            compiler_params=pltpu.CompilerParams(has_side_effects=True, vmem_limit_bytes=60 * 2 ** 20),
            name="reduce_adam_gather",
        )(sc, *big, tail, *state)
        outs = pl.pallas_call(
            unpack_kernel,
            out_shape=tuple(jax.ShapeDtypeStruct((b - a, 128), BF16) for a, b, _ in TENSORS)
            + (jax.ShapeDtypeStruct((TAIL_ROWS, 128), BF16),),
            in_specs=[any_spec],
            out_specs=(any_spec,) * 6,
            scratch_shapes=[pltpu.VMEM((12, NR, 128), BF16), dma((12,)), dma((12, 2))],
            compiler_params=pltpu.CompilerParams(vmem_limit_bytes=40 * 2 ** 20),
            name="unpack",
        )(ag)
        wb = [untiles(o, tt[2], s) for o, tt, s in zip(outs[:5], TENSORS, shapes)]
        flat = outs[5].reshape(-1)
        n1, n2 = g_bqkv.size, g_b1.size
        wb += [flat[:n1].reshape(g_bqkv.shape[1:]), flat[n1:n1 + n2].reshape(g_b1.shape[1:]),
               flat[n1 + n2:n1 + n2 + g_dvec.size].reshape(g_dvec.shape[1:])]
        new = [out3[k].reshape(-1)[:SHARD] for k in range(3)]
        return tuple(new) + tuple(wb)

    g3 = P(AXES, None, None)
    g4 = P(AXES, None, None, None)
    flat = P(AXES)
    rep = P()
    in_specs = (g3, g4, g4, g4, g4, g3, g3, g4, flat, flat, flat, rep, rep, rep, rep, rep)
    out_specs = (flat, flat, flat, rep, rep, rep, rep, rep, rep, rep, rep)
    return jax.shard_map(body, mesh=mesh, in_specs=in_specs, out_specs=out_specs, check_vma=False)
```

time: 949 us -> 246 us (0.26)
  waiting for transfers between devices: 798 us -> 0 us
  Pallas kernels: 0 us -> 229 us
  local copies, waits for them, and re-layouts: 127 us -> 10.2 us
  between operations: 17.6 us -> 4.1 us
    unnamed x4 -> x0, waiting for transfers between devices: 798 us -> none
    pallas_call x0 -> x2, Pallas kernels: none -> 229 us  [the longest x1 216 us: body(): pl.pallas_call(comm_kernel, out_shape=(jax.ShapeDtypeStruct((2, 2, 2, 2,...]
    reshape x13 -> x4, local copies, waits for them, and re-layouts: 59.9 us -> 4.69 us  [the longest x2 4.06 us: body(): jnp.pad(a, (0, LROWS * 128 - SHARD)).reshape(LROWS, 128)]
    unnamed x32 -> x8, local copies, waits for them, and re-layouts: 50 us -> 1.23 us
    slice x9 -> x1, local copies, waits for them, and re-layouts: 15.4 us -> 0.01 us  [body(): flat[n1 + n2:n1 + n2 + g_dvec.size].reshape(g_dvec.shape[1:])]
  transfers between devices with their start and end apart: 2 -> 0, of which waited for: 2 -> 0; matrix products, arithmetic and copies ran while one was open for 0% -> 0% of each run, Pallas kernels for 0% -> 0%
where the time goes in v1:
time: 246 us
  Pallas kernels  229 us (93%)
  local copies, waits for them, and re-layouts  10.2 us (4%)
  between operations  4.1 us (2%)
  other arithmetic  2.82 us (1%)
    pallas_call x1, Pallas kernels, body(): pl.pallas_call(comm_kernel, out_shape=(jax.ShapeDtypeStruct((2, 2, 2, 2,...  216 us
    pallas_call x1, Pallas kernels, body(): pl.pallas_call(unpack_kernel, out_shape=tuple((jax.ShapeDtypeStruct((b -...  12.4 us

profile of v1, /device:TPU:0, one launch (start us, length us, event | category | flops | bytes accessed | tf_op | source)
XLA Modules:
  0.0 245.7 jit_solution(4137308404505304234)
XLA Ops:
  4.1 0.6 stack.35.sc_ref
  4.7 0.7 reduce
  5.4 0.8 reduce.1
  6.2 1.3 fusion.t_ref
  7.5 0.0 copy-start
  7.5 0.0 copy-start.1
  7.5 2.4 pad_bitcast_fusion.2.m_ref
  9.9 0.0 copy-done
  10.0 0.0 copy-done.1
  10.0 1.6 pad_bitcast_fusion
  11.6 216.2 %reduce_adam_gather.1 = (bf16[2,2,2,2,2,2128,128]{6,5,4,3,2,1,0:T(8,128)(2,1)}, f32[3,2120,128]{2,1,0:T(8,128)}) custom-call(f32[8]{0:T(128)} %stack.35.sc_ref, f32[24576,128]{1,0:T(8,128)} %bitcast.92, f32[13824,128]{1,0:T(8,128)} %bitcast.93, f32[4608,128]{1,0:T(8,128)} %bitcast.96, f32[12288,128]{1,0:T(8,128)} %bitcast.94, f32[12288,128]{1,0:T(8,128)} %bitcast.95, ...), custom_call_target="tpu_custom_call" | custom-call | tf_op jit(solution)/shard_map/reduce_adam_gather/pallas_call | solution.py:523
  227.8 3.7 %slice_bitcast_fusion = (f32[271360]{0:T(1024)}, f32[271360]{0:T(1024)}, f32[271360]{0:T(1024)}) fusion(f32[3,2120,128]{2,1,0:T(8,128)} %get-tuple-element.19), kind=kLoop, calls=%fused_computation | loop fusion | bytes 6512640 | tf_op jit(solution)/shard_map/reshape;squeeze | solution.py:553
  231.4 12.4 %unpack.1 = (bf16[24576,128]{1,0:T(8,128)(2,1)}, bf16[13824,128]{1,0:T(8,128)(2,1)}, bf16[4608,128]{1,0:T(8,128)(2,1)}, bf16[12288,128]{1,0:T(8,128)(2,1)}, bf16...) custom-call(bf16[2,2,2,2,2,2128,128]{6,5,4,3,2,1,0:T(8,128)(2,1)} %get-tuple-element.20.ag), custom_call_target="tpu_custom_call" | custom-call | tf_op jit(solution)/shard_map/unpack/pallas_call | solution.py:538
  243.9 0.6 copy.32
  244.5 0.6 reshape.148
  245.1 0.6 copy.31
  (4 shorter events, 0.0 us)
Async XLA Ops:
  7.5 2.4 copy-start
  7.5 2.4 copy-start.1

commit v2 on v1

--- a/solution.py
+++ b/solution.py
@@ -31,6 +31,7 @@
 LOCPAD = 24
 LROWS = 2120
 FROWS = 2464
+SROWS = 2176
 
 
 def win_start(r):
@@ -86,10 +87,10 @@
 NST = len(ORDERS[0])
 
 
-def comm_kernel(sc_ref, e_ref, q_ref, o_ref, w1_ref, w2_ref, t_ref, m_ref, v_ref, w_ref, ag, out3, *scratch):
+def comm_kernel(sc_ref, e_ref, q_ref, o_ref, w1_ref, w2_ref, t_ref, m_ref, v_ref, w_ref, ag, m_out, v_out, w_out, *scratch):
     bufs, scratch = scratch[:3 * NST], scratch[3 * NST:]
-    (S, R0, LOC, F, TIL, HP, HN, GT, GP, GN, FG, WB,
-     ld, s0s, s0r, rss, rsr, ags, agr, fws, fwr, lcl, mvs, hs, hr, osem) = scratch
+    (S, R0, F, TIL, HP, HN, GT, GP, GN, FG,
+     ld, s0s, s0r, rss, rsr, ags, agr, fws, fwr, hs, hr) = scratch
     z = lax.axis_index(AXES[0])
     inner = lax.axis_index(AXES[1])
     h, l, y, x, c = bits(z, 2) + bits(inner, 3)
@@ -97,6 +98,7 @@
     r = z * 8 + inner
     g_refs = (e_ref, q_ref, o_ref, w1_ref, w2_ref, t_ref)
     sc = [sc_ref[i] for i in range(8)]
+    state = (m_ref, v_ref, w_ref)
 
     def flip(ax):
         p = [1 - b if i == ax else b for i, b in enumerate(me)]
@@ -191,8 +193,7 @@
     def ag_copy(k, st, q, recv):
         s = lax.rem(q, SL)
         dst = ag.at[where_ag(k, st, q, recv, c)]
-        src = WB.at[part(k, q)] if st == 0 else dst
-        return remote(src, dst, ags.at[k, st, s], agr.at[k, st, s], PEER[ORDERS[k][NST - 1 - st]])
+        return remote(dst, dst, ags.at[k, st, s], agr.at[k, st, s], PEER[ORDERS[k][NST - 1 - st]])
 
     def fw_copy(k, st, q, core):
         s = lax.rem(q, SL)
@@ -209,9 +210,6 @@
 
         cp.start()
 
-    def own_copy(q):
-        return pltpu.make_async_copy(WB.at[al(q * CH, CH)], ag.at[me + (c, al(q * CH, CH))], lcl.at[lax.rem(q, SL)])
-
     def reduce_stage(k, st, q):
         rs_copy(k, st, q).wait_recv()
         s = lax.rem(q, SL)
@@ -238,30 +236,20 @@
         return [remote(F.at[:, al(nb - HALO, HALO + 16)], HP, hs.at[0], hr.at[0], NXT),
                 remote(F.at[:, pl.ds(HALO, HALO + 16)], HN, hs.at[1], hr.at[1], PRV)]
 
-    def state_copies():
-        return [pltpu.make_async_copy(ref, LOC.at[k, pl.ds(LOCPAD, LROWS)], mvs.at[k])
-                for k, ref in enumerate((m_ref, v_ref, w_ref))]
-
     def shift(ref, at, other, by, keep):
-        a = pltpu.roll(ref[pl.ds(at, 8), :], by, 1)
-        b = pltpu.roll(ref[pl.ds(at + other, 8), :], by, 1)
-        return jnp.where(keep, a, b)
-
-    def prepare1():
-        for cp in state_copies():
-            cp.wait()
-        keep = lane >= delta
+        return pltpu.roll(jnp.where(keep, ref[pl.ds(at, 8), :], ref[pl.ds(at + other, 8), :]), by, 1)
+
+    def prepare1(lo, hi):
+        keep = lane < 128 - delta
 
         def one(i, _):
             for j in range(4):
                 at = i * 32 + j * 8
                 for k in range(3):
-                    F[k, al(HALO + at, 8), :] = shift(LOC.at[k], LOCPAD + at - drow, -1, delta, keep)
+                    F[k, al(HALO + at, 8), :] = shift(state[k], LOCPAD + at - drow, -1, delta, keep)
             return 0
 
-        lax.fori_loop(0, (NR + 16) // 32, one, 0)
-        for cp in halo_copies():
-            cp.start()
+        lax.fori_loop(lo, hi, one, 0)
 
     def blocks(first, last, body):
         for a, b, wt in TENSORS + ((TAIL0, TAIL0 + TAIL_ROWS, 1),):
@@ -293,10 +281,11 @@
 
         lax.fori_loop(0, HALO // 16, one, 0)
 
+    def prepare3(ks):
         def permute(row, wt):
             at = row - sr + HALO
             for j in range(wt):
-                for k in range(3):
+                for k in ks:
                     TIL[k, al(at + 8 * j, 8), :] = (
                         F[k, pl.ds(at + j, 8, stride=wt), :] if wt > 1 else F[k, al(at, 8), :])
 
@@ -305,10 +294,6 @@
     def ghalo_copies():
         return [remote(GT.at[al(nb - HALO, HALO)], GP, hs.at[2], hr.at[2], NXT),
                 remote(GT.at[pl.ds(HALO, HALO + 16)], GN, hs.at[3], hr.at[3], PRV)]
-
-    def finish1():
-        for cp in ghalo_copies():
-            cp.start()
 
     def finish2():
         for cp in ghalo_copies():
@@ -332,29 +317,20 @@
 
         blocks(sr, srn + 16, permute)
 
-    def out_copies():
-        return [pltpu.make_async_copy(LOC.at[k, pl.ds(LOCPAD, LROWS)], out3.at[k], osem.at[k]) for k in range(3)]
-
-    def finish3():
+    def finish3(lo, hi):
         back = lax.rem(128 - delta, 128)
-        keep = lane < 128 - delta
 
         def one(i, _):
             for j in range(5):
                 at = i * 40 + j * 8
-                o = al(LOCPAD + at, 8)
-                g = shift(FG, HALO + drow + at, 1, back, keep)
-                new = adam(g, LOC[0, o, :], LOC[1, o, :], LOC[2, o, :], sc)
-                for k in range(3):
-                    LOC[k, o, :] = new[k]
+                g = shift(FG, HALO + drow + at, 1, back, lane >= delta)
+                new = adam(g, *[ref[al(LOCPAD + at, 8), :] for ref in state], sc)
+                for ref, val in zip((m_out, v_out, w_out), new):
+                    ref[al(at, 8), :] = val
             return 0
 
-        lax.fori_loop(0, LROWS // 40, one, 0)
-        for cp in out_copies():
-            cp.start()
-
-    for cp in state_copies():
-        cp.start()
+        lax.fori_loop(lo, hi, one, 0)
+
     for q in range(AHEAD):
         start0(q)
 
@@ -379,10 +355,6 @@
                 start(rs_copy(k, 0, q), q)
 
         at_stage(0, first)
-
-        @pl.when(s == 1)
-        def _():
-            prepare1()
 
         for st in range(1, NST):
             def middle(q, st=st):
@@ -391,10 +363,6 @@
                     start(rs_copy(k, st, q), q)
 
             at_stage(st, middle)
-
-        @pl.when(s == 2)
-        def _():
-            prepare2()
 
         def update(q):
             for k in range(3):
@@ -406,11 +374,10 @@
                 g = S[me + (o,)] * (1.0 / DEV)
                 GT[oh, :] = g
                 _, _, w2 = adam(g, TIL[0, oh, :], TIL[1, oh, :], TIL[2, oh, :], sc)
-                WB[o, :] = w2.astype(BF16)
+                ag[me + (c, o)] = w2.astype(BF16)
                 return 0
 
             lax.fori_loop(0, CH // 16, one, 0)
-            own_copy(q).start()
             for k in range(3):
                 start(ag_copy(k, 0, q, False), q)
 
@@ -418,8 +385,6 @@
 
         for st in range(NST):
             def gather(q, st=st):
-                if st == 0:
-                    own_copy(q).wait()
                 for k in range(3):
                     ag_copy(k, st, q, True).wait_recv()
                     if st + 1 < NST:
@@ -436,8 +401,24 @@
 
         at_stage(2 * NST + 1, last)
 
-        for n, f in enumerate((finish1, finish2, finish3)):
-            @pl.when(s == K + NST - 1 + n)
+        def send_halos(copies):
+            for cp in copies():
+                cp.start()
+
+        half, done, outer = (NR + 16) // 64, K + NST - 1, LROWS // 40
+        extra = {
+            0: lambda: prepare1(0, half),
+            1: lambda: (prepare1(half, (NR + 16) // 32), send_halos(halo_copies)),
+            2: lambda: (prepare2(), prepare3((0,))),
+            3: lambda: prepare3((1, 2)),
+            done: lambda: send_halos(ghalo_copies),
+            done + 1: finish2,
+        }
+        cuts = [outer * i // NST for i in range(NST + 1)]
+        for i in range(NST):
+            extra[done + 2 + i] = lambda i=i: finish3(cuts[i], cuts[i + 1])
+        for n, f in extra.items():
+            @pl.when(s == n)
             def _(f=f):
                 f()
 
@@ -455,42 +436,22 @@
         return 0
 
     lax.fori_loop(0, SL, drain, 0)
-    for cp in out_copies():
-        cp.wait()
-
-
-def unpack_kernel(ag, e_out, q_out, o_out, w1_out, w2_out, t_out, buf, isem, osem):
+
+
+def unpack_kernel(ag, e_out, q_out, o_out, w1_out, w2_out, t_out, sem):
     outs = (e_out, q_out, o_out, w1_out, w2_out, t_out)
-    depth = buf.shape[0]
-
-    def get(r):
-        return pltpu.make_async_copy(ag.at[tuple(r >> i & 1 for i in (4, 3, 2, 1, 0))], buf.at[r % depth], isem.at[r % depth])
-
-    def puts(r):
+    cps = []
+    for r in range(DEV):
         end = min(win_start(r + 1), TAIL0 + TAIL_ROWS) - win_start(r) if r + 1 < DEV else NR
-        cps = []
-        for n, (i, a, b, size) in enumerate(rows_of(r)):
+        for i, a, b, size in rows_of(r):
             size = min(size, end - b)
             if size > 0:
-                cps.append(pltpu.make_async_copy(buf.at[r % depth, pl.ds(b, size)], outs[i].at[pl.ds(a, size)],
-                                                 osem.at[r % depth, n]))
-        return cps
-
-    for r in range(depth - 2):
-        get(r).start()
-    for r in range(DEV):
-        get(r).wait()
-        for cp in puts(r):
-            cp.start()
-        n = r + depth - 2
-        if n < DEV:
-            if n - depth >= 0:
-                for cp in puts(n - depth):
-                    cp.wait()
-            get(n).start()
-    for r in range(max(0, DEV - depth), DEV):
-        for cp in puts(r):
-            cp.wait()
+                src = ag.at[tuple(r >> j & 1 for j in (4, 3, 2, 1, 0)) + (pl.ds(b, size),)]
+                cps.append(pltpu.make_async_copy(src, outs[i].at[pl.ds(a, size)], sem.at[len(cps)]))
+    for cp in cps:
+        cp.start()
+    for cp in cps:
+        cp.wait()
 
 
 def tiles(x, wt):
@@ -505,6 +466,7 @@
 
 def solution(mesh):
     any_spec = pl.BlockSpec(memory_space=pl.ANY)
+    vmem_spec = pl.BlockSpec(memory_space=pltpu.VMEM)
     dma = pltpu.SemaphoreType.DMA
 
     def vmem(*shape, dtype=F32):
@@ -519,30 +481,32 @@
         t = step.astype(F32)
         sc = jnp.stack([lr, beta1, 1.0 - beta1, beta2, 1.0 - beta2,
                         1.0 / (1.0 - beta1 ** t), 1.0 / (1.0 - beta2 ** t), eps])
-        state = [jnp.pad(a, (0, LROWS * 128 - SHARD)).reshape(LROWS, 128) for a in (m, v, w)]
-        ag, out3 = pl.pallas_call(
+        front = LOCPAD * 128
+        state = [pltpu.with_memory_space_constraint(
+            jnp.pad(a, (front, SROWS * 128 - front - SHARD)).reshape(SROWS, 128), pltpu.VMEM) for a in (m, v, w)]
+        ag, *new = pl.pallas_call(
             comm_kernel,
-            out_shape=(jax.ShapeDtypeStruct((2, 2, 2, 2, 2, NR, 128), BF16), jax.ShapeDtypeStruct((3, LROWS, 128), F32)),
-            in_specs=[pl.BlockSpec(memory_space=pltpu.SMEM)] + [any_spec] * 9,
-            out_specs=(any_spec, any_spec),
+            out_shape=(pltpu.VMEM((2, 2, 2, 2, 2, NR, 128), BF16),) + (pltpu.VMEM((LROWS, 128), F32),) * 3,
+            in_specs=[pl.BlockSpec(memory_space=pltpu.SMEM)] + [any_spec] * 6 + [vmem_spec] * 3,
+            out_specs=(vmem_spec,) * 4,
             scratch_shapes=[vmem(SL, *[2] * (NST - 1 - st), n) for n in PARTS for st in range(NST)] + [
                 vmem(2, 2, 2, 2, NR), vmem(S0, 2, 2, 2, 2, CH),
-                vmem(3, 2176), vmem(3, FROWS), vmem(3, FROWS), vmem(3, HALO + 16), vmem(3, HALO + 16),
-                vmem(NR + 2 * HALO), vmem(HALO), vmem(HALO + 16), vmem(NR + 2 * HALO), vmem(NR, dtype=BF16),
+                vmem(3, FROWS), vmem(3, FROWS), vmem(3, HALO + 16), vmem(3, HALO + 16),
+                vmem(NR + 2 * HALO), vmem(HALO), vmem(HALO + 16), vmem(NR + 2 * HALO),
                 dma((S0,)), dma((S0,)), dma((S0,))] + [dma((3, NST, SL)) for _ in range(6)] + [
-                dma((SL,)), dma((3,)), dma((4,)), dma((4,)), dma((3,)),
+                dma((4,)), dma((4,)),
             ],
-            compiler_params=pltpu.CompilerParams(has_side_effects=True, vmem_limit_bytes=60 * 2 ** 20),
+            compiler_params=pltpu.CompilerParams(has_side_effects=True, vmem_limit_bytes=36 * 2 ** 20),
             name="reduce_adam_gather",
         )(sc, *big, tail, *state)
         outs = pl.pallas_call(
             unpack_kernel,
             out_shape=tuple(jax.ShapeDtypeStruct((b - a, 128), BF16) for a, b, _ in TENSORS)
             + (jax.ShapeDtypeStruct((TAIL_ROWS, 128), BF16),),
-            in_specs=[any_spec],
+            in_specs=[vmem_spec],
             out_specs=(any_spec,) * 6,
-            scratch_shapes=[pltpu.VMEM((12, NR, 128), BF16), dma((12,)), dma((12, 2))],
-            compiler_params=pltpu.CompilerParams(vmem_limit_bytes=40 * 2 ** 20),
+            scratch_shapes=[dma((DEV + 8,))],
+            compiler_params=pltpu.CompilerParams(vmem_limit_bytes=20 * 2 ** 20),
             name="unpack",
         )(ag)
         wb = [untiles(o, tt[2], s) for o, tt, s in zip(outs[:5], TENSORS, shapes)]
@@ -550,7 +514,7 @@
         n1, n2 = g_bqkv.size, g_b1.size
         wb += [flat[:n1].reshape(g_bqkv.shape[1:]), flat[n1:n1 + n2].reshape(g_b1.shape[1:]),
                flat[n1 + n2:n1 + n2 + g_dvec.size].reshape(g_dvec.shape[1:])]
-        new = [out3[k].reshape(-1)[:SHARD] for k in range(3)]
+        new = [a.reshape(-1)[:SHARD] for a in new]
         return tuple(new) + tuple(wb)
 
     g3 = P(AXES, None, None)

time: 246 us -> 233 us (0.947)
  Pallas kernels: 229 us -> 218 us
  local copies, waits for them, and re-layouts: 10.2 us -> 7.65 us
    pallas_call x1, Pallas kernels: 12.4 us -> 6.31 us  [body(): pl.pallas_call(unpack_kernel, out_shape=tuple((jax.ShapeDtypeStruct((b -...]
    pallas_call x1, Pallas kernels: 216 us -> 212 us  [body(): pl.pallas_call(comm_kernel, out_shape=(pltpu.VMEM((2, 2, 2, 2, 2, NR, 128...]
    another operation x1 -> x0, local copies, waits for them, and re-layouts: 3.66 us -> none  [body(): new = [out3[k].reshape(-1)[:SHARD] for k in range(3)]]
    unnamed x8 -> x11, local copies, waits for them, and re-layouts: 1.23 us -> 4.8 us
where the time goes in v2:
time: 233 us
  Pallas kernels  218 us (94%)
  local copies, waits for them, and re-layouts  7.65 us (3%)
  between operations  4.11 us (2%)
  other arithmetic  2.82 us (1%)
    pallas_call x1, Pallas kernels, body(): pl.pallas_call(comm_kernel, out_shape=(pltpu.VMEM((2, 2, 2, 2, 2, NR, 128...  212 us
    pallas_call x1, Pallas kernels, body(): pl.pallas_call(unpack_kernel, out_shape=tuple((jax.ShapeDtypeStruct((b -...  6.31 us
    unnamed x11, local copies, waits for them, and re-layouts  4.8 us

profile of v2, /device:TPU:0, one launch (start us, length us, event | category | flops | bytes accessed | tf_op | source)
XLA Modules:
  0.0 232.7 jit_solution(4231108904234540481)
XLA Ops:
  4.1 0.6 stack.35.sc_ref
  4.7 0.7 reduce
  5.4 0.8 reduce.1
  6.2 1.3 fusion.t_ref
  7.5 0.0 copy-start
  7.5 0.0 copy-start.1
  7.5 1.5 pad_bitcast_fusion.2.m_ref
  9.0 0.1 copy-done
  9.1 0.3 copy-done.1
  9.4 0.1 pad_bitcast_fusion
  9.5 211.8 %reduce_adam_gather.1 = (bf16[2,2,2,2,2,2128,128]{6,5,4,3,2,1,0:T(8,128)(2,1)S(1)}, f32[2120,128]{1,0:T(8,128)S(1)}, f32[2120,128]{1,0:T(8,128)S(1)}, f32[2120,128]{1,0:T(8,128)S(1)}) custom-call(f32[8]{0:T(128)} %stack.35.sc_ref, f32[24576,128]{1,0:T(8,128)} %bitcast.92, f32[13824,128]{1,0:T(8,128)} %bitcast.93, f32[4608,128]{1,0:T(8,128)} %bitcast.96, ...), custom_call_target="tpu_custom_call" | custom-call | tf_op jit(solution)/shard_map/reduce_adam_gather/pallas_call | solution.py:487
  221.4 6.3 %unpack.1 = (bf16[24576,128]{1,0:T(8,128)(2,1)}, bf16[13824,128]{1,0:T(8,128)(2,1)}, bf16[4608,128]{1,0:T(8,128)(2,1)}, bf16[12288,128]{1,0:T(8,128)(2,1)}, bf16...) custom-call(bf16[2,2,2,2,2,2128,128]{6,5,4,3,2,1,0:T(8,128)(2,1)S(1)} %get-tuple-element.24.ag), custom_call_target="tpu_custom_call" | custom-call | tf_op jit(solution)/shard_map/unpack/pallas_call | solution.py:502
  227.7 0.6 copy.32
  228.3 0.6 reshape.160
  229.0 0.6 copy.31
  229.6 1.1 copy.41
  230.6 1.1 copy.42
  231.7 1.1 copy.43
  (4 shorter events, 0.0 us)
Async XLA Ops:
  7.5 1.6 copy-start
  7.5 1.9 copy-start.1

commit v3 on v2

--- a/solution.py
+++ b/solution.py
@@ -50,6 +50,15 @@
     return segs
 
 
+def halo_rows(n):
+    s = win_start(n)
+    for a, b, wt in TENSORS + ((TAIL0, TAIL0 + TAIL_ROWS, 1),):
+        if a <= s < b:
+            first = a + (s - a) // (8 * wt) * 8 * wt
+            end = first + 8 * wt
+    return s + 16 - first // 16 * 16, max(16, -(-end // 16) * 16 - s) if first < s else 16
+
+
 def al(i, n, a=8):
     return pl.ds(pl.multiple_of(i, a), n)
 
@@ -232,9 +241,24 @@
     lane = lax.broadcasted_iota(jnp.int32, (8, 128), 1)
     sub = lax.broadcasted_iota(jnp.int32, (8, 128), 0)
 
-    def halo_copies():
-        return [remote(F.at[:, al(nb - HALO, HALO + 16)], HP, hs.at[0], hr.at[0], NXT),
-                remote(F.at[:, pl.ds(HALO, HALO + 16)], HN, hs.at[1], hr.at[1], PRV)]
+    def halo_up(n):
+        size, _ = halo_rows(n)
+        o = pl.ds(HALO + 16 - size, size)
+        return remote(F.at[:, al(nb + 16 - size, size)], HP.at[:, o], hs.at[0], hr.at[0], NXT)
+
+    def halo_down(n):
+        _, size = halo_rows(n)
+        return remote(F.at[:, pl.ds(HALO, size)], HN.at[:, pl.ds(0, size)], hs.at[1], hr.at[1], PRV)
+
+    def halos(sent, received):
+        for n in range(DEV):
+            @pl.when(r == n)
+            def _(n=n):
+                for cp in [halo_up(n + 1)] * (n + 1 < DEV) + [halo_down(n)] * (n > 0):
+                    sent(cp)
+                if received is not None:
+                    for cp in [halo_down(n + 1)] * (n + 1 < DEV) + [halo_up(n)] * (n > 0):
+                        received(cp)
 
     def shift(ref, at, other, by, keep):
         return pltpu.roll(jnp.where(keep, ref[pl.ds(at, 8), :], ref[pl.ds(at + other, 8), :]), by, 1)
@@ -263,8 +287,7 @@
             lax.fori_loop(lo, hi, one, 0)
 
     def prepare2():
-        for cp in halo_copies():
-            cp.wait()
+        halos(lambda cp: cp.wait_send(), lambda cp: cp.wait_recv())
         for k in range(3):
             for i in range(0, 16, 8):
                 idx = (sub + i) * 128 + lane
@@ -331,8 +354,17 @@
 
         lax.fori_loop(lo, hi, one, 0)
 
+    barrier = pltpu.get_barrier_semaphore()
+    friends = PEER + [CORE, NXT, PRV]
+    for dev in friends:
+        pl.semaphore_signal(barrier, inc=1, device_id=dev, device_id_type=MESH)
+    pl.semaphore_wait(barrier, len(friends))
     for q in range(AHEAD):
         start0(q)
+    turns, edge_turns = (NR + 16) // 32, (HALO + 32) // 32
+    prepare1(0, edge_turns)
+    prepare1(turns - edge_turns, turns)
+    halos(lambda cp: cp.start(), None)
 
     def step(s, _):
         def at_stage(n, body):
@@ -401,17 +433,17 @@
 
         at_stage(2 * NST + 1, last)
 
-        def send_halos(copies):
-            for cp in copies():
+        def send_halos():
+            for cp in ghalo_copies():
                 cp.start()
 
-        half, done, outer = (NR + 16) // 64, K + NST - 1, LROWS // 40
+        done, outer = K + NST - 1, LROWS // 40
         extra = {
-            0: lambda: prepare1(0, half),
-            1: lambda: (prepare1(half, (NR + 16) // 32), send_halos(halo_copies)),
+            0: lambda: prepare1(edge_turns, turns // 2),
+            1: lambda: prepare1(turns // 2, turns - edge_turns),
             2: lambda: (prepare2(), prepare3((0,))),
             3: lambda: prepare3((1, 2)),
-            done: lambda: send_halos(ghalo_copies),
+            done: send_halos,
             done + 1: finish2,
         }
         cuts = [outer * i // NST for i in range(NST + 1)]
@@ -438,16 +470,17 @@
     lax.fori_loop(0, SL, drain, 0)
 
 
-def unpack_kernel(ag, e_out, q_out, o_out, w1_out, w2_out, t_out, sem):
+def unpack_kernel(ag, m_new, v_new, w_new, e_out, q_out, o_out, w1_out, w2_out, t_out, m_out, v_out, w_out, sem):
     outs = (e_out, q_out, o_out, w1_out, w2_out, t_out)
-    cps = []
+    cps = [pltpu.make_async_copy(src, dst, sem.at[DEV + 8 + k])
+           for k, (src, dst) in enumerate(((m_new, m_out), (v_new, v_out), (w_new, w_out)))]
     for r in range(DEV):
         end = min(win_start(r + 1), TAIL0 + TAIL_ROWS) - win_start(r) if r + 1 < DEV else NR
         for i, a, b, size in rows_of(r):
             size = min(size, end - b)
             if size > 0:
                 src = ag.at[tuple(r >> j & 1 for j in (4, 3, 2, 1, 0)) + (pl.ds(b, size),)]
-                cps.append(pltpu.make_async_copy(src, outs[i].at[pl.ds(a, size)], sem.at[len(cps)]))
+                cps.append(pltpu.make_async_copy(src, outs[i].at[pl.ds(a, size)], sem.at[len(cps) - 3]))
     for cp in cps:
         cp.start()
     for cp in cps:
@@ -496,26 +529,25 @@
                 dma((S0,)), dma((S0,)), dma((S0,))] + [dma((3, NST, SL)) for _ in range(6)] + [
                 dma((4,)), dma((4,)),
             ],
-            compiler_params=pltpu.CompilerParams(has_side_effects=True, vmem_limit_bytes=36 * 2 ** 20),
+            compiler_params=pltpu.CompilerParams(has_side_effects=True, collective_id=0, vmem_limit_bytes=36 * 2 ** 20),
             name="reduce_adam_gather",
         )(sc, *big, tail, *state)
         outs = pl.pallas_call(
             unpack_kernel,
             out_shape=tuple(jax.ShapeDtypeStruct((b - a, 128), BF16) for a, b, _ in TENSORS)
-            + (jax.ShapeDtypeStruct((TAIL_ROWS, 128), BF16),),
-            in_specs=[vmem_spec],
-            out_specs=(any_spec,) * 6,
-            scratch_shapes=[dma((DEV + 8,))],
-            compiler_params=pltpu.CompilerParams(vmem_limit_bytes=20 * 2 ** 20),
+            + (jax.ShapeDtypeStruct((TAIL_ROWS, 128), BF16),) + (jax.ShapeDtypeStruct((SHARD,), F32),) * 3,
+            in_specs=[vmem_spec] * 4,
+            out_specs=(any_spec,) * 9,
+            scratch_shapes=[dma((DEV + 11,))],
+            compiler_params=pltpu.CompilerParams(vmem_limit_bytes=2 ** 20),
             name="unpack",
-        )(ag)
+        )(ag, *[a.reshape(-1)[:SHARD] for a in new])
         wb = [untiles(o, tt[2], s) for o, tt, s in zip(outs[:5], TENSORS, shapes)]
         flat = outs[5].reshape(-1)
         n1, n2 = g_bqkv.size, g_b1.size
         wb += [flat[:n1].reshape(g_bqkv.shape[1:]), flat[n1:n1 + n2].reshape(g_b1.shape[1:]),
                flat[n1 + n2:n1 + n2 + g_dvec.size].reshape(g_dvec.shape[1:])]
-        new = [a.reshape(-1)[:SHARD] for a in new]
-        return tuple(new) + tuple(wb)
+        return tuple(outs[6:]) + tuple(wb)
 
     g3 = P(AXES, None, None)
     g4 = P(AXES, None, None, None)

time: 233 us -> 222 us (0.953)
  Pallas kernels: 218 us -> 211 us
  local copies, waits for them, and re-layouts: 7.65 us -> 4.49 us
    pallas_call x1, Pallas kernels: 212 us -> 203 us  [body(): pl.pallas_call(comm_kernel, out_shape=(pltpu.VMEM((2, 2, 2, 2, 2, NR, 128...]
    unnamed x11 -> x8, local copies, waits for them, and re-layouts: 4.8 us -> 1.64 us
where the time goes in v3:
time: 222 us
  Pallas kernels  211 us (95%)
  local copies, waits for them, and re-layouts  4.49 us (2%)
  between operations  4.11 us (2%)
  other arithmetic  2.82 us (1%)
    pallas_call x1, Pallas kernels, body(): pl.pallas_call(comm_kernel, out_shape=(pltpu.VMEM((2, 2, 2, 2, 2, NR, 128...  203 us
    pallas_call x1, Pallas kernels, body(): pl.pallas_call(unpack_kernel, out_shape=tuple((jax.ShapeDtypeStruct((b -...  7.31 us

profile of v3, /device:TPU:0, one launch (start us, length us, event | category | flops | bytes accessed | tf_op | source)
XLA Modules:
  0.0 222.1 jit_solution(5441300081681036274)
XLA Ops:
  4.1 0.6 stack.35.sc_ref
  4.7 0.7 reduce
  5.4 0.8 reduce.1
  6.2 1.3 fusion.t_ref
  7.5 0.0 copy-start
  7.5 0.0 copy-start.1
  7.5 1.5 pad_bitcast_fusion.2.m_ref
  9.0 0.1 copy-done
  9.1 0.3 copy-done.1
  9.4 0.1 pad_bitcast_fusion
  9.5 203.3 %reduce_adam_gather.1 = (bf16[2,2,2,2,2,2128,128]{6,5,4,3,2,1,0:T(8,128)(2,1)S(1)}, f32[2120,128]{1,0:T(8,128)S(1)}, f32[2120,128]{1,0:T(8,128)S(1)}, f32[2120,128]{1,0:T(8,128)S(1)}) custom-call(f32[8]{0:T(128)} %stack.35.sc_ref, f32[24576,128]{1,0:T(8,128)} %bitcast.92, f32[13824,128]{1,0:T(8,128)} %bitcast.93, f32[4608,128]{1,0:T(8,128)} %bitcast.96, ...), custom_call_target="tpu_custom_call" | custom-call | tf_op jit(solution)/shard_map/reduce_adam_gather/pallas_call | solution.py:520
  212.9 7.3 %unpack.1 = (bf16[24576,128]{1,0:T(8,128)(2,1)}, bf16[13824,128]{1,0:T(8,128)(2,1)}, bf16[4608,128]{1,0:T(8,128)(2,1)}, bf16[12288,128]{1,0:T(8,128)(2,1)}, bf16...) custom-call(bf16[2,2,2,2,2,2128,128]{6,5,4,3,2,1,0:T(8,128)(2,1)S(1), ...), custom_call_target="tpu_custom_call" | custom-call | tf_op jit(solution)/shard_map/unpack/pallas_call | solution.py:535
  220.2 0.6 copy.32
  220.8 0.6 reshape.160
  221.5 0.6 copy.31
  (4 shorter events, 0.0 us)
Async XLA Ops:
  7.5 1.6 copy-start
  7.5 1.9 copy-start.1

commit v4 on v3

--- a/solution.py
+++ b/solution.py
@@ -22,8 +22,8 @@
 LAST_ROW = 67654
 NR = 2128
 K = 19
-NA, NB, NC = 40, 48, 24
-CH = NA + NB + NC
+PARTS = (40, 40, 16, 16)
+CH = sum(PARTS)
 SL = 4
 S0 = 5
 AHEAD = 2
@@ -90,16 +90,30 @@
 
 
 H, L, Y, X = range(4)
-ORDERS = ((X, Y, L, H), (Y, X, L, H), (L, H, X, Y))
-PARTS = (NA, NB, NC)
-STARTS = (0, NA, NA + NB)
+IN, MID, OUT = range(4, 7)
+LINE = (IN, MID, OUT)
+ORDERS = ((X, Y) + LINE, (Y, X) + LINE, LINE + (X, Y), LINE + (Y, X))
+COLOURS = range(len(ORDERS))
+STARTS = tuple(sum(PARTS[:k]) for k in COLOURS)
 NST = len(ORDERS[0])
+PIECES = [(k, st, p) for k in COLOURS for st in range(NST) for p in range(2 if ORDERS[k][st] == IN else 1)]
+
+
+def free_axes(k, st, p):
+    o = ORDERS[k]
+    kind = o[st]
+    free = [ax for ax in (Y, X) if o.index(ax) > st]
+    if kind in (Y, X):
+        free += [H, L] * (o.index(IN) > st)
+    elif kind == MID or kind == IN and p == 1:
+        free.append(L)
+    return sorted(free)
 
 
 def comm_kernel(sc_ref, e_ref, q_ref, o_ref, w1_ref, w2_ref, t_ref, m_ref, v_ref, w_ref, ag, m_out, v_out, w_out, *scratch):
-    bufs, scratch = scratch[:3 * NST], scratch[3 * NST:]
+    bufs, scratch = dict(zip(PIECES, scratch)), scratch[len(PIECES):]
     (S, R0, F, TIL, HP, HN, GT, GP, GN, FG,
-     ld, s0s, s0r, rss, rsr, ags, agr, fws, fwr, hs, hr) = scratch
+     ld, s0s, s0r, rss, rsr, ags, agr, fws, fwr, ows, owr, hs, hr) = scratch
     z = lax.axis_index(AXES[0])
     inner = lax.axis_index(AXES[1])
     h, l, y, x, c = bits(z, 2) + bits(inner, 3)
@@ -109,11 +123,14 @@
     sc = [sc_ref[i] for i in range(8)]
     state = (m_ref, v_ref, w_ref)
 
-    def flip(ax):
-        p = [1 - b if i == ax else b for i, b in enumerate(me)]
+    end = h == l
+    middle = h != l
+
+    def flip(*axes):
+        p = [1 - b if i in axes else b for i, b in enumerate(me)]
         return p[H] * 2 + p[L], p[Y] * 4 + p[X] * 2 + c
 
-    PEER = [flip(ax) for ax in range(4)]
+    PEER = {X: flip(X), Y: flip(Y), IN: flip(L), OUT: flip(L), MID: flip(H, L)}
     CORE = (z, inner + 1 - 2 * c)
 
     def device(i):
@@ -178,39 +195,56 @@
     def part(k, q):
         return al(q * CH + STARTS[k], PARTS[k])
 
-    def where_rs(k, st, q, other):
-        o = ORDERS[k]
-        idx = [every] * 4
-        for ax in o[:st]:
-            idx[ax] = me[ax]
-        idx[o[st]] = 1 - me[o[st]] if other else me[o[st]]
-        return idx + [part(k, q)]
-
-    def where_ag(k, st, q, other, core):
-        o = ORDERS[k][::-1]
-        idx = list(me)
-        for ax in o[:st]:
-            idx[ax] = every
-        idx[o[st]] = 1 - me[o[st]] if other else me[o[st]]
-        return tuple(idx + [core, part(k, q)])
-
-    def rs_copy(k, st, q):
+    def piece(k, st, p):
+        kind = ORDERS[k][st]
+        away, home = list(me), list(me)
+        for ax in free_axes(k, st, p):
+            away[ax] = home[ax] = every
+        if kind in (Y, X):
+            away[kind] = 1 - me[kind]
+            return away, home, None, None
+        if kind == MID:
+            away[H] = 1 - h
+            return away, home, middle, middle
+        if kind == OUT:
+            away[L] = 1 - l
+            return away, home, middle, end
+        if p == 0:
+            away[L] = 1 - l
+        else:
+            away[H] = home[H] = 1 - h
+        return away, home, end, middle
+
+    def by(role, body):
+        if role is None:
+            body()
+        else:
+            pl.when(role)(body)
+
+    def sem(kp):
+        return PIECES.index(kp)
+
+    def rs_copy(kp, q):
+        s, i = lax.rem(q, SL), sem(kp)
+        away = piece(*kp)[0]
+        return remote(S.at[tuple(away) + (part(kp[0], q),)], bufs[kp].at[s], rss.at[i, s], rsr.at[i, s],
+                      PEER[ORDERS[kp[0]][kp[1]]])
+
+    def ag_copy(kp, q, recv):
+        s, i = lax.rem(q, SL), sem(kp)
+        idx = piece(*kp)[0 if recv else 1]
+        ref = ag.at[tuple(idx) + (c, part(kp[0], q))]
+        return remote(ref, ref, ags.at[i, s], agr.at[i, s], PEER[ORDERS[kp[0]][kp[1]]])
+
+    def fw_copy(kp, q, core):
+        s, i = lax.rem(q, SL), sem(kp)
+        ref = ag.at[tuple(piece(*kp)[0]) + (core, part(kp[0], q))]
+        return remote(ref, ref, fws.at[i, s], fwr.at[i, s], CORE)
+
+    def own_copy(q, core):
         s = lax.rem(q, SL)
-        return remote(S.at[tuple(where_rs(k, st, q, True))], bufs[k * NST + st].at[s],
-                      rss.at[k, st, s], rsr.at[k, st, s], PEER[ORDERS[k][st]])
-
-    def ag_copy(k, st, q, recv):
-        s = lax.rem(q, SL)
-        dst = ag.at[where_ag(k, st, q, recv, c)]
-        return remote(dst, dst, ags.at[k, st, s], agr.at[k, st, s], PEER[ORDERS[k][NST - 1 - st]])
-
-    def fw_copy(k, st, q, core):
-        s = lax.rem(q, SL)
-        idx = list(where_ag(k, st, q, True, core))
-        if st == 0:
-            idx[ORDERS[k][NST - 1]] = every
-        ref = ag.at[tuple(idx)]
-        return remote(ref, ref, fws.at[k, st, s], fwr.at[k, st, s], CORE)
+        ref = ag.at[me + (core, al(q * CH, CH))]
+        return remote(ref, ref, ows.at[s], owr.at[s], CORE)
 
     def start(cp, q):
         @pl.when(q >= SL)
@@ -219,19 +253,48 @@
 
         cp.start()
 
-    def reduce_stage(k, st, q):
-        rs_copy(k, st, q).wait_recv()
-        s = lax.rem(q, SL)
-        idx = where_rs(k, st, q, False)
-        free = ORDERS[k][st + 1:]
-
-        def dst(w):
-            at = list(idx)
-            for ax, b in zip(sorted(free), bits(w, len(free))):
-                at[ax] = b
-            return S.at[tuple(at)]
-
-        loop_add(dst, lambda w: bufs[k * NST + st].at[(s,) + bits(w, len(free))], 2 ** len(free), PARTS[k])
+    def at(st, k=None):
+        return [kp for kp in PIECES if kp[1] == st and k in (None, kp[0])]
+
+    def rs_start(st, q, k=None):
+        for kp in at(st, k):
+            by(piece(*kp)[2], lambda kp=kp: start(rs_copy(kp, q), q))
+
+    def ag_start(st, q, k=None):
+        for kp in at(st, k):
+            by(piece(*kp)[3], lambda kp=kp: start(ag_copy(kp, q, False), q))
+
+    def rs_finish(st, q, k):
+        for kp in at(st, k):
+            _, home, _, gets = piece(*kp)
+            free = free_axes(*kp)
+
+            def dst(w, home=home, free=free):
+                to = list(home)
+                for ax, bit in zip(free, bits(w, len(free))):
+                    to[ax] = bit
+                return S.at[tuple(to) + (part(k, q),)]
+
+            def src(w, kp=kp, free=free):
+                return bufs[kp].at[(lax.rem(q, SL),) + bits(w, len(free))]
+
+            def body(kp=kp, dst=dst, src=src, free=free):
+                rs_copy(kp, q).wait_recv()
+                loop_add(dst, src, 2 ** len(free), PARTS[k])
+
+            by(gets, body)
+
+    def ag_finish(st, q, k):
+        for kp in at(st, k):
+            by(piece(*kp)[2], lambda kp=kp: ag_copy(kp, q, True).wait_recv())
+
+    def fw_start(st, q, k):
+        for kp in at(st, k):
+            by(piece(*kp)[2], lambda kp=kp: start(fw_copy(kp, q, c), q))
+
+    def fw_finish(st, q, k):
+        for kp in at(st, k):
+            by(piece(*kp)[2], lambda kp=kp: fw_copy(kp, q, 1 - c).wait_recv())
 
     sr, srn = win_start(r), win_start(r + 1)
     delta = lax.rem(r * 24, 128)
@@ -355,7 +418,7 @@
         lax.fori_loop(lo, hi, one, 0)
 
     barrier = pltpu.get_barrier_semaphore()
-    friends = PEER + [CORE, NXT, PRV]
+    friends = [PEER[X], PEER[Y], PEER[IN], PEER[MID], CORE, NXT, PRV]
     for dev in friends:
         pl.semaphore_signal(barrier, inc=1, device_id=dev, device_id_type=MESH)
     pl.semaphore_wait(barrier, len(friends))
@@ -383,22 +446,21 @@
 
             slot = lax.rem(q, S0)
             loop_add(lambda w: S.at[bits(w, 4) + (al(q * CH, CH),)], lambda w: R0.at[(slot,) + bits(w, 4)], 16, CH)
-            for k in range(3):
-                start(rs_copy(k, 0, q), q)
+            rs_start(0, q)
 
         at_stage(0, first)
 
         for st in range(1, NST):
             def middle(q, st=st):
-                for k in range(3):
-                    reduce_stage(k, st - 1, q)
-                    start(rs_copy(k, st, q), q)
+                for k in COLOURS:
+                    rs_finish(st - 1, q, k)
+                    rs_start(st, q, k)
 
             at_stage(st, middle)
 
         def update(q):
-            for k in range(3):
-                reduce_stage(k, NST - 1, q)
+            for k in COLOURS:
+                rs_finish(NST - 1, q, k)
 
             def one(i, _):
                 o = al(q * CH + i * 16, 16)
@@ -410,26 +472,28 @@
                 return 0
 
             lax.fori_loop(0, CH // 16, one, 0)
-            for k in range(3):
-                start(ag_copy(k, 0, q, False), q)
+            ag_start(NST - 1, q)
+            start(own_copy(q, c), q)
 
         at_stage(NST, update)
 
         for st in range(NST):
-            def gather(q, st=st):
-                for k in range(3):
-                    ag_copy(k, st, q, True).wait_recv()
+            def gather(q, st=NST - 1 - st):
+                if st == NST - 1:
+                    own_copy(q, 1 - c).wait_recv()
+                for k in COLOURS:
+                    ag_finish(st, q, k)
+                    if st:
+                        ag_start(st - 1, q, k)
                     if st + 1 < NST:
-                        start(ag_copy(k, st + 1, q, False), q)
-                    if st:
-                        fw_copy(k, st - 1, q, 1 - c).wait_recv()
-                    start(fw_copy(k, st, q, c), q)
+                        fw_finish(st + 1, q, k)
+                    fw_start(st, q, k)
 
             at_stage(NST + 1 + st, gather)
 
         def last(q):
-            for k in range(3):
-                fw_copy(k, NST - 1, q, 1 - c).wait_recv()
+            for k in COLOURS:
+                fw_finish(0, q, k)
 
         at_stage(2 * NST + 1, last)
 
@@ -460,11 +524,12 @@
 
     def drain(i, _):
         q = K - SL + i
-        for k in range(3):
-            for st in range(NST):
-                rs_copy(k, st, q).wait_send()
-                ag_copy(k, st, q, False).wait_send()
-                fw_copy(k, st, q, c).wait_send()
+        own_copy(q, c).wait_send()
+        for kp in PIECES:
+            _, _, away, home = piece(*kp)
+            by(away, lambda kp=kp: rs_copy(kp, q).wait_send())
+            by(away, lambda kp=kp: fw_copy(kp, q, c).wait_send())
+            by(home, lambda kp=kp: ag_copy(kp, q, False).wait_send())
         return 0
 
     lax.fori_loop(0, SL, drain, 0)
@@ -522,14 +587,14 @@
             out_shape=(pltpu.VMEM((2, 2, 2, 2, 2, NR, 128), BF16),) + (pltpu.VMEM((LROWS, 128), F32),) * 3,
             in_specs=[pl.BlockSpec(memory_space=pltpu.SMEM)] + [any_spec] * 6 + [vmem_spec] * 3,
             out_specs=(vmem_spec,) * 4,
-            scratch_shapes=[vmem(SL, *[2] * (NST - 1 - st), n) for n in PARTS for st in range(NST)] + [
+            scratch_shapes=[vmem(SL, *[2] * len(free_axes(*kp)), PARTS[kp[0]]) for kp in PIECES] + [
                 vmem(2, 2, 2, 2, NR), vmem(S0, 2, 2, 2, 2, CH),
                 vmem(3, FROWS), vmem(3, FROWS), vmem(3, HALO + 16), vmem(3, HALO + 16),
                 vmem(NR + 2 * HALO), vmem(HALO), vmem(HALO + 16), vmem(NR + 2 * HALO),
-                dma((S0,)), dma((S0,)), dma((S0,))] + [dma((3, NST, SL)) for _ in range(6)] + [
-                dma((4,)), dma((4,)),
+                dma((S0,)), dma((S0,)), dma((S0,))] + [dma((len(PIECES), SL)) for _ in range(6)] + [
+                dma((SL,)), dma((SL,)), dma((4,)), dma((4,)),
             ],
-            compiler_params=pltpu.CompilerParams(has_side_effects=True, collective_id=0, vmem_limit_bytes=36 * 2 ** 20),
+            compiler_params=pltpu.CompilerParams(has_side_effects=True, collective_id=0, vmem_limit_bytes=38 * 2 ** 20),
             name="reduce_adam_gather",
         )(sc, *big, tail, *state)
         outs = pl.pallas_call(

time: 222 us -> 215 us (0.968)
  Pallas kernels: 211 us -> 203 us
    pallas_call x1, Pallas kernels: 203 us -> 196 us  [body(): pl.pallas_call(comm_kernel, out_shape=(pltpu.VMEM((2, 2, 2, 2, 2, NR, 128...]
where the time goes in v4:
time: 215 us
  Pallas kernels  203 us (94%)
  local copies, waits for them, and re-layouts  4.49 us (2%)
  between operations  4.11 us (2%)
  other arithmetic  2.82 us (1%)
    pallas_call x1, Pallas kernels, body(): pl.pallas_call(comm_kernel, out_shape=(pltpu.VMEM((2, 2, 2, 2, 2, NR, 128...  196 us
    pallas_call x1, Pallas kernels, body(): pl.pallas_call(unpack_kernel, out_shape=tuple((jax.ShapeDtypeStruct((b -...  7.31 us

profile of v4, /device:TPU:0, one launch (start us, length us, event | category | flops | bytes accessed | tf_op | source)
XLA Modules:
  0.0 214.8 jit_solution(18255166001890183492)
XLA Ops:
  4.1 0.6 stack.35.sc_ref
  4.7 0.7 reduce
  5.4 0.8 reduce.1
  6.2 1.3 fusion.t_ref
  7.5 0.0 copy-start
  7.5 0.0 copy-start.1
  7.5 1.5 pad_bitcast_fusion.2.m_ref
  9.0 0.1 copy-done
  9.1 0.3 copy-done.1
  9.4 0.1 pad_bitcast_fusion
  9.5 196.1 %reduce_adam_gather.1 = (bf16[2,2,2,2,2,2128,128]{6,5,4,3,2,1,0:T(8,128)(2,1)S(1)}, f32[2120,128]{1,0:T(8,128)S(1)}, f32[2120,128]{1,0:T(8,128)S(1)}, f32[2120,128]{1,0:T(8,128)S(1)}) custom-call(f32[8]{0:T(128)} %stack.35.sc_ref, f32[24576,128]{1,0:T(8,128)} %bitcast.92, f32[13824,128]{1,0:T(8,128)} %bitcast.93, f32[4608,128]{1,0:T(8,128)} %bitcast.96, ...), custom_call_target="tpu_custom_call" | custom-call | tf_op jit(solution)/shard_map/reduce_adam_gather/pallas_call | solution.py:585
  205.6 7.3 %unpack.1 = (bf16[24576,128]{1,0:T(8,128)(2,1)}, bf16[13824,128]{1,0:T(8,128)(2,1)}, bf16[4608,128]{1,0:T(8,128)(2,1)}, bf16[12288,128]{1,0:T(8,128)(2,1)}, bf16...) custom-call(bf16[2,2,2,2,2,2128,128]{6,5,4,3,2,1,0:T(8,128)(2,1)S(1), ...), custom_call_target="tpu_custom_call" | custom-call | tf_op jit(solution)/shard_map/unpack/pallas_call | solution.py:600
  213.0 0.6 copy.32
  213.6 0.6 reshape.160
  214.2 0.6 copy.31
  (4 shorter events, 0.0 us)
Async XLA Ops:
  7.5 1.6 copy-start
  7.5 1.9 copy-start.1

commit v5 on v4

--- a/solution.py
+++ b/solution.py
@@ -574,8 +574,8 @@
         grads = (g_emb, g_qkv, g_o, g_w1, g_w2)
         shapes = tuple(g.shape[1:] for g in grads)
         big = [tiles(g, t[2]) for g, t in zip(grads, TENSORS)]
-        tail = jnp.concatenate([g_bqkv.reshape(-1), g_b1.reshape(-1), g_dvec.reshape(-1)])
-        tail = jnp.pad(tail, (0, TAIL_ROWS * 128 - tail.shape[0])).reshape(TAIL_ROWS, 128)
+        tail = jnp.concatenate([g.reshape(1, -1) for g in (g_bqkv, g_b1, g_dvec)], axis=1)
+        tail = jnp.pad(tail, ((0, 0), (0, TAIL_ROWS * 128 - tail.shape[1]))).reshape(TAIL_ROWS, 128)
         t = step.astype(F32)
         sc = jnp.stack([lr, beta1, 1.0 - beta1, beta2, 1.0 - beta2,
                         1.0 / (1.0 - beta1 ** t), 1.0 / (1.0 - beta2 ** t), eps])

time: 215 us -> 214 us (level)
  no operation moved by 1% of the time
where the time goes in v5:
time: 214 us; the launch traced here: 213 us
  Pallas kernels  203 us (95%)
  local copies, waits for them, and re-layouts  4.49 us (2%)
  between operations  4.1 us (2%)
    pallas_call x1, Pallas kernels, body(): pl.pallas_call(comm_kernel, out_shape=(pltpu.VMEM((2, 2, 2, 2, 2, NR, 128...  196 us
    pallas_call x1, Pallas kernels, body(): pl.pallas_call(unpack_kernel, out_shape=tuple((jax.ShapeDtypeStruct((b -...  7.31 us

profile of v5, /device:TPU:0, one launch (start us, length us, event | category | flops | bytes accessed | tf_op | source)
XLA Modules:
  0.0 213.4 jit_solution(11164907294374916154)
XLA Ops:
  4.1 0.6 stack.35.sc_ref
  4.7 1.4 select_maximum_fusion
  6.0 0.0 copy-start
  6.0 0.0 copy-start.1
  6.1 1.5 pad_bitcast_fusion.2.m_ref
  7.5 0.1 copy-done
  7.6 0.3 copy-done.1
  7.9 0.1 pad_bitcast_fusion
  8.1 196.1 %reduce_adam_gather.1 = (bf16[2,2,2,2,2,2128,128]{6,5,4,3,2,1,0:T(8,128)(2,1)S(1)}, f32[2120,128]{1,0:T(8,128)S(1)}, f32[2120,128]{1,0:T(8,128)S(1)}, f32[2120,128]{1,0:T(8,128)S(1)}) custom-call(f32[8]{0:T(128)} %stack.35.sc_ref, f32[24576,128]{1,0:T(8,128)} %bitcast.93, f32[13824,128]{1,0:T(8,128)} %bitcast.94, f32[4608,128]{1,0:T(8,128)} %bitcast.97, ...), custom_call_target="tpu_custom_call" | custom-call | tf_op jit(solution)/shard_map/reduce_adam_gather/pallas_call | solution.py:585
  204.2 7.3 %unpack.1 = (bf16[24576,128]{1,0:T(8,128)(2,1)}, bf16[13824,128]{1,0:T(8,128)(2,1)}, bf16[4608,128]{1,0:T(8,128)(2,1)}, bf16[12288,128]{1,0:T(8,128)(2,1)}, bf16...) custom-call(bf16[2,2,2,2,2,2128,128]{6,5,4,3,2,1,0:T(8,128)(2,1)S(1), ...), custom_call_target="tpu_custom_call" | custom-call | tf_op jit(solution)/shard_map/unpack/pallas_call | solution.py:600
  211.5 0.6 copy.32
  212.1 0.6 reshape.160
  212.7 0.6 copy.31
  (3 shorter events, 0.0 us)
Async XLA Ops:
  6.0 1.6 copy-start
  6.0 1.9 copy-start.1
